TPU v7x, 8 devices: a whole 2x2x1 slice. The times are simulated.
8 devices in a mesh: tp: 2 (over z, y), dp: 2 (over x), pp: 2 (over core).
Axes of the slice: x: 2, y: 2, z: 1, core: 2. Of those that a mesh axis runs over, the one named last changes fastest.
Arguments:
- master: float32 [32000, 1152], P('tp')
- exp_avg: float32 [32000, 1152], P('tp')
- exp_avg_sq: float32 [32000, 1152], P('tp')
- stage_ids: int32 [2, 12, 768], P('pp', 'dp')
- stage_acts: bfloat16 [2, 12, 768, 1152], P('pp', 'dp')
Outputs:
- output 1: float32 [32000, 1152], P('tp')
- output 2: float32 [32000, 1152], P('tp')
- output 3: float32 [32000, 1152], P('tp')
- output 4: bfloat16 [32000, 1152], P('tp')
All inputs are finite; a program needn't handle non-finite values.
Results may differ from a plain program's by a relative error of at most 0.001.
Values sent between devices are 32-bit elements.
A program may use at most 2 GiB of HBM per device.

v0:
```python
import functools

import jax
import jax.numpy as jnp
from jax import lax
from jax.experimental import pallas as pl
from jax.experimental.pallas import tpu as pltpu
from jax.sharding import PartitionSpec as P


LEARN_RATE = 0.003
BETA_ONE = 0.9
BETA_TWO = 0.95
ADAM_EPS = 1e-8
WEIGHT_DECAY = 0.1
CLIP_NORM = 1.0
OPT_STEP = 10
VMEM_CAP = 63 * 1024 * 1024
F32 = jnp.float32
BF16 = jnp.bfloat16
AXES = ("tp", "dp", "pp")
ANY = pl.ANY


def params(n_axes=1):
    return pltpu.CompilerParams(dimension_semantics=("arbitrary",) * n_axes, vmem_limit_bytes=VMEM_CAP)


def logits_kernel(n_sub, starts, stage_ref, *refs):
    n_src = len(starts)
    fa_refs, fb_refs, e_ref = refs[:n_src], refs[n_src : 2 * n_src], refs[2 * n_src]
    lg_ref, f_ref, m_ref, z_ref = refs[-4:]
    t = pl.program_id(0)

    @pl.when(pl.program_id(1) == 0)
    def _():
        for j in range(n_src):
            here = t >= starts[j]
            if j + 1 < n_src:
                here = jnp.logical_and(here, t < starts[j + 1])

            @pl.when(jnp.logical_and(here, stage_ref[0] == 1))
            def _(j=j):
                f_ref[...] = fa_refs[j][...].astype(BF16)

            @pl.when(jnp.logical_and(here, stage_ref[0] == 0))
            def _(j=j):
                f_ref[...] = fb_refs[j][...].astype(BF16)

        m_ref[...] = jnp.full_like(m_ref, -jnp.inf)
        z_ref[...] = jnp.zeros_like(z_ref)

    width = f_ref.shape[0] // n_sub
    for j in range(n_sub):
        cols = slice(j * width, (j + 1) * width)
        lg_ref[:, cols] = lax.dot_general(e_ref[...], f_ref[cols, :], (((1,), (1,)), ((), ())), preferred_element_type=F32)
        m_old = m_ref[:, cols]
        m_new = jnp.maximum(m_old, jnp.max(lg_ref[:, cols], axis=0, keepdims=True))
        part = jnp.sum(jnp.exp(lg_ref[:, cols] - m_new), axis=0, keepdims=True)
        z_ref[:, cols] = z_ref[:, cols] * jnp.exp(m_old - m_new) + part
        m_ref[:, cols] = m_new


def logits_call(stage, srcs, e_bf, t_blk, tb, vb, tok, prev):
    vq, d = e_bf.shape
    first = prev is None
    starts, n_t = [], 0
    for src in srcs:
        starts.append(n_t)
        n_t += src[4]

    def src_spec(blk, start, count):
        mode = {"pipeline_mode": pl.Buffered(1)} if count == 1 else {}
        return pl.BlockSpec((tb, d), lambda t, v, s: (blk + jnp.clip(t - start, 0, count - 1), 0), **mode)

    in_specs = [src_spec(src[1], st, src[4]) for src, st in zip(srcs, starts)]
    in_specs += [src_spec(src[3], st, src[4]) for src, st in zip(srcs, starts)]
    in_specs += [pl.BlockSpec((vb, d), lambda t, v, s: (v, 0))]
    in_specs += [] if first else [pl.BlockSpec(memory_space=ANY)] * 2
    out_specs = [
        pl.BlockSpec((vb, tb), lambda t, v, s: (v, t_blk + t)),
        pl.BlockSpec((tb, d), lambda t, v, s: (t_blk + t, 0)),
        pl.BlockSpec((1, tb), lambda t, v, s: (0, t)),
        pl.BlockSpec((1, tb), lambda t, v, s: (0, t)),
    ]
    n_sub = max(1, tb // 256)
    n_in = 2 * len(srcs) + 2
    return pl.pallas_call(
        functools.partial(logits_kernel, n_sub, starts),
        grid_spec=pltpu.PrefetchScalarGridSpec(num_scalar_prefetch=1, grid=(n_t, vq // vb), in_specs=in_specs, out_specs=out_specs),
        out_shape=[
            jax.ShapeDtypeStruct((vq, tok), F32),
            jax.ShapeDtypeStruct((tok, d), BF16),
            jax.ShapeDtypeStruct((1, n_t * tb), F32),
            jax.ShapeDtypeStruct((1, n_t * tb), F32),
        ],
        input_output_aliases={} if first else {n_in: 0, n_in + 1: 1},
        compiler_params=params(2),
        cost_estimate=pl.CostEstimate(
            flops=2 * vq * n_t * tb * d, bytes_accessed=n_t * (2 * vq * d + 4 * vq * tb), transcendentals=vq * n_t * tb
        ),
        name="logits",
    )(stage, *[src[0] for src in srcs], *[src[2] for src in srcs], e_bf, *(() if first else prev))


def grad_body(unit, k_width, lg_ref, f_ref, m_ref, w_ref, lab_ref, g_ref, t, t_width):
    rows = lg_ref.shape[0]
    base = pl.program_id(0) * rows
    for k in range(t_width // k_width):
        cols = slice(k * k_width, (k + 1) * k_width)
        row = lax.broadcasted_iota(jnp.int32, (rows, k_width), 0)
        prob = jnp.exp(lg_ref[:, cols] - m_ref[:, cols]) * w_ref[:, cols]
        dl = (prob - jnp.where(row == lab_ref[:, cols] - base, unit, 0.0)).astype(BF16)
        toks = pl.ds(pl.multiple_of(t * t_width + k * k_width, k_width), k_width)
        g_ref[...] += jnp.dot(dl, f_ref[toks, :], preferred_element_type=F32)


def grad_local_kernel(unit, k_width, lg_ref, f_ref, m_ref, w_ref, lab_ref, g_ref):
    t = pl.program_id(1)

    @pl.when(t == 0)
    def _():
        g_ref[...] = jnp.zeros_like(g_ref)

    grad_body(unit, k_width, lg_ref, f_ref, m_ref, w_ref, lab_ref, g_ref, t, lg_ref.shape[1])


def grad_remote_kernel(unit, k_width, n_pre, off_ref, lg_ref, f_ref, m_ref, w_ref, lab_ref, gin_ref, key_ref, srt_ref, g_ref, sq_ref, buf, sem):
    v, t = pl.program_id(0), pl.program_id(1)
    rows, chunk = g_ref.shape[0], buf.shape[2]
    c_lo = off_ref[v] // chunk
    c_hi = (off_ref[v + 1] + chunk - 1) // chunk
    c_hi = jnp.where(off_ref[v + 1] > off_ref[v], c_hi, c_lo)

    def fetch(c, slot):
        return pltpu.make_async_copy(srt_ref.at[:, pl.ds(pl.multiple_of(c * chunk, chunk), chunk), :], buf.at[slot], sem.at[slot])

    def add_rows(c, slot):
        row = lax.broadcasted_iota(jnp.int32, (rows, chunk), 0)
        hot = jnp.where(row == key_ref[c] - v * rows, 1.0, 0.0).astype(BF16)
        for i in range(3):
            g_ref[...] += jnp.dot(hot, buf[slot, i], preferred_element_type=F32)

    @pl.when(t == 0)
    def _():
        g_ref[...] = gin_ref[...]
        for j in range(n_pre):
            @pl.when(c_lo + j < c_hi)
            def _():
                fetch(c_lo + j, j).start()

    grad_body(unit, k_width, lg_ref, f_ref, m_ref, w_ref, lab_ref, g_ref, t, lg_ref.shape[1])

    @pl.when(t == pl.num_programs(1) - 1)
    def _():
        for j in range(n_pre):
            @pl.when(c_lo + j < c_hi)
            def _():
                fetch(c_lo + j, j).wait()
                add_rows(c_lo + j, j)

        @pl.loop(c_lo + n_pre, c_hi)
        def _(c):
            fetch(c, 0).start()
            fetch(c, 0).wait()
            add_rows(c, 0)

        @pl.when(v == 0)
        def _():
            sq_ref[...] = jnp.zeros_like(sq_ref)

        sq_ref[...] += jnp.sum(g_ref[...] * g_ref[...], axis=0, keepdims=True)


def grad_call(lg, f_bf, peak, weight, lab, unit, vb, tb, k_width, extra=None):
    vq, tok = lg.shape
    d = f_bf.shape[1]
    n_t = tok // tb
    rest = (lambda f: f) if extra is None else (lambda f: (lambda v, t, *_: f(v, t)))
    in_specs = [
        pl.BlockSpec((vb, tb), rest(lambda v, t: (v, t))),
        pl.BlockSpec((tok, d), rest(lambda v, t: (0, 0)), pipeline_mode=pl.Buffered(1)),
        pl.BlockSpec((1, tb), rest(lambda v, t: (0, t))),
        pl.BlockSpec((1, tb), rest(lambda v, t: (0, t))),
        pl.BlockSpec((1, tb), rest(lambda v, t: (0, t))),
    ]
    g_spec = pl.BlockSpec((vb, d), rest(lambda v, t: (v, 0)))
    g_shape = jax.ShapeDtypeStruct((vq, d), F32)
    cost = pl.CostEstimate(flops=2 * vq * tok * d, bytes_accessed=4 * vq * (tok + 2 * d), transcendentals=vq * tok)
    if extra is None:
        return pl.pallas_call(
            functools.partial(grad_local_kernel, unit, k_width),
            grid=(vq // vb, n_t),
            in_specs=in_specs,
            out_specs=g_spec,
            out_shape=g_shape,
            compiler_params=params(2),
            cost_estimate=cost,
            name="grad_local",
        )(lg, f_bf, peak, weight, lab)
    offs, g_in, keys, srt, chunk = extra
    n_pre = 3
    return pl.pallas_call(
        functools.partial(grad_remote_kernel, unit, k_width, n_pre),
        grid_spec=pltpu.PrefetchScalarGridSpec(
            num_scalar_prefetch=1,
            grid=(vq // vb, n_t),
            in_specs=in_specs + [g_spec, pl.BlockSpec(keys.shape, lambda v, t, *_: (0, 0, 0)), pl.BlockSpec(memory_space=ANY)],
            out_specs=[g_spec, pl.BlockSpec((1, d), lambda v, t, *_: (0, 0))],
            scratch_shapes=[pltpu.VMEM((n_pre, 3, chunk, d), BF16), pltpu.SemaphoreType.DMA((n_pre,))],
        ),
        out_shape=[g_shape, jax.ShapeDtypeStruct((1, d), F32)],
        input_output_aliases={6: 0},
        compiler_params=params(2),
        cost_estimate=cost,
        name="grad_remote",
    )(offs, lg, f_bf, peak, weight, lab, g_in, keys, srt)


def distinct_kernel(n_stage_rows, blocks, info_ref, uk_ref, key_ref, *refs):
    n_src = (len(refs) - 4) // 2
    src_a, src_b = refs[:n_src], refs[n_src : 2 * n_src]
    out_ref, dx_ref, buf, sem = refs[-4:]
    c = pl.program_id(0)
    chunk = out_ref.shape[1]
    depth = buf.shape[0]

    @pl.when(c == 0)
    def _():
        def start(i):
            q, row = blocks[i]

            @pl.when(info_ref[1] == 0)
            def _():
                pltpu.make_async_copy(src_a[q].at[pl.ds(row, n_stage_rows), :], buf.at[i % depth], sem.at[i % depth]).start()

            @pl.when(info_ref[1] == 1)
            def _():
                pltpu.make_async_copy(src_b[q].at[pl.ds(row, n_stage_rows), :], buf.at[i % depth], sem.at[i % depth]).start()

        for i in range(min(depth - 1, len(blocks))):
            start(i)
        for i in range(len(blocks)):
            if i + depth - 1 < len(blocks):
                start(i + depth - 1)
            pltpu.make_async_copy(src_a[0].at[pl.ds(0, n_stage_rows), :], buf.at[i % depth], sem.at[i % depth]).wait()
            dx_ref[i * n_stage_rows : (i + 1) * n_stage_rows, :] = buf[i % depth].astype(BF16)

    @pl.when(c < info_ref[0])
    def _():
        n_tok = dx_ref.shape[0]
        width = n_tok // 6
        acc = jnp.zeros((chunk, dx_ref.shape[1]), F32)
        for k in range(6):
            cols = slice(k * width, (k + 1) * width)
            hot = jnp.where(uk_ref[...] == key_ref[:, cols], 1.0, 0.0).astype(BF16)
            acc += jnp.dot(hot, dx_ref[cols, :], preferred_element_type=F32)
        high = acc.astype(BF16)
        rest = acc - high.astype(F32)
        mid = rest.astype(BF16)
        out_ref[0] = high
        out_ref[1] = mid
        out_ref[2] = (rest - mid.astype(F32)).astype(BF16)


def distinct_call(info, uk, key, srcs_a, srcs_b, chunk, n_stage_rows):
    d = srcs_a[0].shape[1]
    blocks = [(q, row) for q, src in enumerate(srcs_a) for row in range(0, src.shape[0], n_stage_rows)]
    cap = uk.shape[0]
    n_tok = key.shape[1]

    def last(c, info_ref):
        return jnp.minimum(c, jnp.maximum(info_ref[0] - 1, 0))

    return pl.pallas_call(
        functools.partial(distinct_kernel, n_stage_rows, blocks),
        grid_spec=pltpu.PrefetchScalarGridSpec(
            num_scalar_prefetch=1,
            grid=(cap // chunk,),
            in_specs=[pl.BlockSpec((chunk, 1), lambda c, i: (last(c, i), 0)), pl.BlockSpec((1, n_tok), lambda c, i: (0, 0))]
            + [pl.BlockSpec(memory_space=ANY)] * (2 * len(srcs_a)),
            out_specs=pl.BlockSpec((3, chunk, d), lambda c, i: (0, last(c, i), 0)),
            scratch_shapes=[pltpu.VMEM((n_tok, d), BF16), pltpu.VMEM((4, n_stage_rows, d), F32), pltpu.SemaphoreType.DMA((4,))],
        ),
        out_shape=jax.ShapeDtypeStruct((3, cap, d), BF16),
        compiler_params=params(),
        cost_estimate=pl.CostEstimate(flops=40_000_000_000, bytes_accessed=n_tok * d * 4, transcendentals=0),
        name="distinct_sums",
    )(info, uk, key, *srcs_a, *srcs_b)


def adamw_kernel(off_ref, scale_ref, e_ref, m_ref, v_ref, g_ref, *rest):
    ne_ref, nm_ref, nv_ref, nb_ref = rest[-4:]
    grad = g_ref[...] * scale_ref[0]
    new_avg = BETA_ONE * m_ref[...] + (1.0 - BETA_ONE) * grad
    new_sq = BETA_TWO * v_ref[...] + (1.0 - BETA_TWO) * grad * grad
    step_dir = (new_avg / (1.0 - BETA_ONE**OPT_STEP)) / (jnp.sqrt(new_sq / (1.0 - BETA_TWO**OPT_STEP)) + ADAM_EPS)
    master = e_ref[...]
    new_master = master - LEARN_RATE * (step_dir + WEIGHT_DECAY * master)
    ne_ref[...] = new_master
    nm_ref[...] = new_avg
    nv_ref[...] = new_sq
    nb_ref[...] = new_master.astype(BF16)


def adamw_call(off, scale, master, exp_avg, exp_avg_sq, grad, vb, prev):
    rows, d = grad.shape
    first = prev is None
    here = pl.BlockSpec((vb, d), lambda i, off_ref, sc: (off_ref[0] + i, 0))
    shape = jax.ShapeDtypeStruct(master.shape, F32)
    return pl.pallas_call(
        adamw_kernel,
        grid_spec=pltpu.PrefetchScalarGridSpec(
            num_scalar_prefetch=2,
            grid=(rows // vb,),
            in_specs=[here, here, here, pl.BlockSpec((vb, d), lambda i, off_ref, sc: (i, 0))]
            + ([] if first else [pl.BlockSpec(memory_space=ANY)] * 4),
            out_specs=[here] * 4,
        ),
        out_shape=[shape, shape, shape, jax.ShapeDtypeStruct(master.shape, BF16)],
        input_output_aliases={} if first else {6: 0, 7: 1, 8: 2, 9: 3},
        compiler_params=params(),
        cost_estimate=pl.CostEstimate(flops=80_000_000_000, bytes_accessed=rows * d * 30, transcendentals=0),
        name="adamw",
    )(off, scale, master, exp_avg, exp_avg_sq, grad, *(() if first else prev))


def permute(x, flip, stage=None):
    pairs = []
    for t in range(2):
        for r in range(2):
            for s in range(2):
                if stage is not None and s != stage:
                    continue
                dst = (t ^ ("tp" in flip), r ^ ("dp" in flip), s ^ ("pp" in flip))
                pairs.append((4 * t + 2 * r + s, 4 * dst[0] + 2 * dst[1] + dst[2]))
    return lax.ppermute(x, AXES, pairs)


def after(x, *deps):
    return lax.optimization_barrier((x,) + deps)[0]


def swap_halves(x):
    half = x.shape[1] // 2
    return jnp.concatenate([x[:, half:], x[:, :half]], axis=1)


def reduce_stats(m, z, far, then):
    mine = jnp.concatenate([m, z], axis=0)
    others = [permute(mine, flip) for flip in ("pp", "tp", "tp pp")]
    others = [after(x, then) for x in others]
    if far:
        others[1:] = [swap_halves(x) for x in others[1:]]
    peak = m
    for x in others:
        peak = jnp.maximum(peak, x[0:1])
    total = z * jnp.exp(m - peak)
    for x in others:
        total = total + x[1:2] * jnp.exp(x[0:1] - peak)
    return peak, total


def solution(mesh):
    assert all(mesh.shape[a] == 2 for a in AXES)
    table_spec = P("tp", None)

    def stage_step(master, exp_avg, exp_avg_sq, stage_ids, stage_acts):
        tp, _, pp = (lax.axis_index(a) for a in AXES)
        v_dev, d = master.shape
        vq = v_dev // 2
        tok = stage_ids.shape[1] * stage_ids.shape[2]
        half = tok // 2
        tb = tok // 6
        dxb = half // 2
        vb1, vb2, vb3 = vq // 5, vq // 10, vq // 20
        chunk = 256
        stage = pp.astype(jnp.int32).reshape(1)
        act = stage_acts.reshape(tok, d)
        ids = stage_ids.reshape(1, tok)

        def part(source, start, size):
            return lax.dynamic_slice(source, (start, 0), (size, d)).astype(F32)

        zero = lax.optimization_barrier(jnp.int32(0))
        fx = [lax.optimization_barrier(part(act, tp * half, 2 * tb))]
        fx.append(lax.optimization_barrier(part(after(act, fx[0]), tp * half + 2 * tb, tb)))
        own = [lax.optimization_barrier(part(after(act, fx[0], fx[1]), zero, tb))]
        own.append(lax.optimization_barrier(part(after(act, own[0]), zero + tb, tok - tb)))
        e_bf = lax.dynamic_slice(after(master, own[1]), (pp * vq, 0), (vq, d)).astype(BF16)
        sib = [permute(own[0], "pp"), permute(own[1], "pp")]
        fx = [permute(fx[0], "dp", 1), permute(fx[1], "dp", 1)]

        lg_a = logits_call(stage, [(act, 0, sib[0], 0, 1)], e_bf, 0, tb, vb1, tok, None)
        lg_b = logits_call(stage, [(act, 1, sib[1], 0, 2)], e_bf, 1, tb, vb1, tok, lg_a[:2])
        fx0 = after(fx[0], lg_b[2])
        fy0, fxs0 = permute(fx0, "tp", 1), permute(fx0, "pp", 1)
        act_b = after(act, lg_b[2])
        dx = [permute(lax.optimization_barrier(part(act_b, tp * half + k * dxb, dxb)), "dp", 0) for k in range(2)]
        lg_c = logits_call(stage, [(act, 3, sib[1], 2, 3)], e_bf, 3, tb, vb1, tok, lg_b[:2])
        fx1 = after(fx[1], lg_c[2])
        fy1, fxs1 = permute(fx1, "tp", 1), permute(fx1, "pp", 1)

        sib_ids, far_ids, far_sib = (permute(ids, flip) for flip in ("pp", "dp", "dp pp"))
        sib_ids, far_ids, far_sib = (after(x, lg_c[2]) for x in (sib_ids, far_ids, far_sib))
        near = jnp.concatenate([jnp.where(pp == 0, ids, sib_ids), jnp.where(pp == 0, sib_ids, ids)], axis=0)
        far = jnp.concatenate([jnp.where(pp == 0, far_ids, far_sib), jnp.where(pp == 0, far_sib, far_ids)], axis=0)
        far = jnp.where(tp == 0, far, swap_halves(far))
        all_ids = jnp.concatenate([near, far], axis=1) - (2 * tp + pp) * vq

        key = all_ids[0]
        key = jnp.where(jnp.logical_and(key >= 0, key < vq), key, vq)
        srt = lax.sort(key)
        new = jnp.concatenate([srt[:1] < vq, jnp.logical_and(srt[1:] != srt[:-1], srt[1:] < vq)])
        cap = min(-(-vq // chunk) * chunk, 2 * tok)
        uk = lax.sort(jnp.where(new, srt, 2 * vq))[:cap]
        edges = jnp.arange(vq // vb2 + 1, dtype=jnp.int32) * vb2
        offs = jnp.sum((uk[None, :] < edges[:, None]).astype(jnp.int32), axis=1)
        info = jnp.stack([(offs[-1] + chunk - 1) // chunk, pp.astype(jnp.int32)])

        src = [(after(fx[0], lg_c[2]), 0, after(fxs0, lg_c[2]), 0, 2)]
        fr_a = logits_call(stage, src, e_bf, 0, tb, vb1, tok, None)
        m_loc, z_loc = reduce_stats(*(jnp.concatenate([lg_a[i], lg_b[i], lg_c[i]], axis=1) for i in (2, 3)), False, fr_a[2])
        fys0, fys1 = permute(after(fy0, fr_a[2]), "pp", 1), permute(after(fy1, fr_a[2]), "pp", 1)
        dx0 = after(dx[0], fr_a[2])
        dy0, dxs0 = permute(dx0, "tp", 0), permute(dx0, "pp", 0)
        unit = 1.0 / tok
        lg_loc = after(lg_c[0], fr_a[2])
        g_loc = grad_call(lg_loc, lg_c[1], m_loc, unit / z_loc, all_ids[1:2, :tok], unit, vb2, tok // 2, tb)
        dx1 = after(dx[1], g_loc)
        dy1, dxs1 = permute(dx1, "tp", 0), permute(dx1, "pp", 0)
        dys0 = permute(after(dy0, g_loc), "pp", 0)
        e_far = after(e_bf, g_loc)
        rest = [(after(fx1, g_loc), 0, after(fxs1, g_loc), 0, 1), (after(fy0, g_loc), 0, after(fys0, g_loc), 0, 2)]
        rest.append((after(fy1, g_loc), 0, after(fys1, g_loc), 0, 1))
        fr_b = logits_call(stage, rest, e_far, 2, tb, vb1, tok, fr_a[:2])
        dys1 = permute(after(dy1, fr_b[2]), "pp", 0)
        srcs = own + [dx[0], dx[1], dy0, dy1], sib + [after(dxs0, fr_b[2]), after(dxs1, fr_b[2]), after(dys0, fr_b[2]), dys1]
        sums = distinct_call(info, uk.reshape(-1, 1), key.reshape(1, -1), *srcs, chunk, tb // 2)
        m_far, z_far = reduce_stats(*(jnp.concatenate([fr_a[i], fr_b[i]], axis=1) for i in (2, 3)), True, sums)
        extra = (offs, g_loc, uk.reshape(-1, 1, chunk), sums, chunk)
        grad, sq = grad_call(fr_b[0], fr_b[1], m_far, unit / z_far, all_ids[1:2, tok:], unit, vb2, tok // 2, tb, extra)

        other = permute(grad, "pp")
        sq_total = lax.psum(jnp.sum(sq), ("tp", "pp")) * 0.25
        scale = (0.5 * (CLIP_NORM / jnp.maximum(jnp.sqrt(sq_total), CLIP_NORM))).reshape(1)
        n_blk = vq // vb3
        outs = adamw_call(stage * n_blk, scale, master, exp_avg, exp_avg_sq, grad, vb3, None)
        return tuple(adamw_call((1 - stage) * n_blk, scale, master, exp_avg, exp_avg_sq, other, vb3, outs))

    return jax.shard_map(
        stage_step,
        mesh=mesh,
        in_specs=(table_spec, table_spec, table_spec, P("pp", "dp", None), P("pp", "dp", None, None)),
        out_specs=(table_spec, table_spec, table_spec, table_spec),
        check_vma=False,
    )
```

profile of v0, /device:TPU:0, one launch (start us, length us, event | category | flops | bytes accessed | tf_op | source)
XLA Modules:
  0.0 1045.3 jit_solution(11668961848290335901)
XLA Ops:
  0.6 5.4 dynamic-slice_convert_fusion.2
  6.1 3.5 dynamic-slice_convert_fusion.6
  11.3 12.4 %dynamic-slice_convert_fusion.1.refs_1_ = f32[3840,1152]{1,0:T(8,128)} fusion(bf16[4608,1152]{1,0:T(8,128)(2,1)} %bitcast.12, s32[]{:T(128)S(6)} %select_n.66), kind=kLoop, calls=%fused_computation.1 | loop fusion | flops 4423680 | bytes 26542084 | tf_op jit(solution)/shard_map/convert_element_type | solution.py:383
  24.5 3.5 collective-permute-start.6
  28.0 3.0 collective-permute-start.3
  31.0 19.9 %dynamic-slice_convert_fusion.refs_2_.refs_6_ = bf16[8000,1152]{1,0:T(8,128)(2,1)} fusion(f32[16000,1152]{1,0:T(8,128)} %e_ref.3, s32[]{:T(128)S(6)} %select_n.67), kind=kLoop, calls=%fused_computation | loop fusion | bytes 36864004 | tf_op jit(solution)/shard_map/convert_element_type | solution.py:390
  50.9 5.1 collective-permute-done.2.refs_1_.refs_6_
  56.4 26.5 %logits.5 = (f32[8000,4608]{1,0:T(8,128)}, bf16[4608,1152]{1,0:T(8,128)(2,1)}, f32[1,768]{1,0:T(1,128)}, f32[1,768]{1,0:T(1,128)}) custom-call(s32[1]{0:T(128)} %bitcast.stage_ref, bf16[4608,1152]{1,0:T(8,128)(2,1)} %bitcast.13, f32[768,1152]{1,0:T(8,128)} %collective-permute-done.2.refs_1_.refs_6_, bf16[8000,1152]{1,0:T(8,128)(2,1)} %dynamic-slice_convert_fusion.refs_2_.refs_6_), custom_call_target="tpu_custom_call" | custom-call | flops 14155776000 | bytes 43008000 | tf_op jit(solution)/shard_map/logits/pallas_call | solution.py:88
  86.0 48.8 %logits.6 = (f32[8000,4608]{1,0:T(8,128)}, bf16[4608,1152]{1,0:T(8,128)(2,1)}, f32[1,1536]{1,0:T(1,128)}, f32[1,1536]{1,0:T(1,128)}) custom-call(s32[1]{0:T(128)} %bitcast.stage_ref, bf16[4608,1152]{1,0:T(8,128)(2,1)} %bitcast.14, f32[3840,1152]{1,0:T(8,128)} %collective-permute-done.1.refs_1_.refs_7_, ...), custom_call_target="tpu_custom_call", output_to_operand_aliasing={{0}: (4, {}), {1}: (5, {})} | custom-call | flops 28311552000 | bytes 86016000 | tf_op jit(solution)/shard_map/logits/pallas_call | solution.py:88
  136.3 71.2 %logits.7 = (f32[8000,4608]{1,0:T(8,128)}, bf16[4608,1152]{1,0:T(8,128)(2,1)}, f32[1,2304]{1,0:T(1,128)}, f32[1,2304]{1,0:T(1,128)}) custom-call(s32[1]{0:T(128)} %bitcast.stage_ref, bf16[4608,1152]{1,0:T(8,128)(2,1)} %bitcast.15, f32[3840,1152]{1,0:T(8,128)} %collective-permute-done.1.refs_1_.refs_7_, ...), custom_call_target="tpu_custom_call", output_to_operand_aliasing={{0}: (4, {}), {1}: (5, {})} | custom-call | flops 42467328000 | bytes 129024000 | tf_op jit(solution)/shard_map/logits/pallas_call | solution.py:88
  207.6 5.6 dynamic-slice_convert_fusion.3
  213.2 3.5 collective-permute-start.11
  216.7 4.5 collective-permute-start.17
  228.8 50.8 %collective-permute-done.17.refs_2_ = f32[1152,1152]{1,0:T(8,128)S(1)} collective-permute-done((f32[1152,1152]{1,0:T(8,128)S(1)}, f32[1152,1152]{1,0:T(8,128)S(1)}, u32[]{:S(2)}, u32[]{:S(2)}) %collective-permute-start.17) | collective-permute-done | bytes 5308448 | tf_op jit(solution)/shard_map/ppermute | solution.py:337
  282.0 50.8 %logits.8 = (f32[8000,4608]{1,0:T(8,128)}, bf16[4608,1152]{1,0:T(8,128)(2,1)}, f32[1,1536]{1,0:T(1,128)}, f32[1,1536]{1,0:T(1,128)}) custom-call(s32[1]{0:T(128)} %bitcast.stage_ref, f32[1536,1152]{1,0:T(8,128)} %collective-permute-done.6.refs_0_, f32[1536,1152]{1,0:T(8,128)} %collective-permute-done.7.refs_1_, ...), custom_call_target="tpu_custom_call" | custom-call | flops 28311552000 | bytes 86016000 | tf_op jit(solution)/shard_map/logits/pallas_call | solution.py:88
  334.2 3.9 collective-permute-start.18
  339.4 3.4 collective-permute-start.19
  345.3 117.7 %grad_local.1.gin_ref = f32[8000,1152]{1,0:T(8,128)} custom-call(f32[8000,4608]{1,0:T(8,128)} %get-tuple-element.90.lg_ref, bf16[4608,1152]{1,0:T(8,128)(2,1)} %get-tuple-element.91.f_ref, f32[1,4608]{1,0:T(1,128)} %get-tuple-element.135.m_ref, f32[1,4608]{1,0:T(1,128)} %get-tuple-element.134.w_ref, s32[1,4608]{1,0:T(1,128)} %get-tuple-element.139.lab_ref), custom_call_target="tpu_custom_call" | custom-call | flops 84934656000 | bytes 221184000 | tf_op jit(solution)/shard_map/grad_local/pallas_call | solution.py:191
  463.0 13.6 %collective-permute-start.22 = (f32[1152,1152]{1,0:T(8,128)}, f32[1152,1152]{1,0:T(8,128)}, u32[]{:S(2)}, u32[]{:S(2)}) collective-permute-start(f32[1152,1152]{1,0:T(8,128)} %collective-permute-done.18.refs_3_), channel_id=1, source_target_pairs={{0,1},{2,3},{4,5},{6,7}} | collective-permute-start | bytes 15925256 | tf_op jit(solution)/shard_map/ppermute | solution.py:337
  476.6 3.6 collective-permute-start.20
  480.3 3.6 collective-permute-start.21
  483.9 3.7 collective-permute-start.23
  487.6 96.3 %logits.9 = (f32[8000,4608]{1,0:T(8,128)}, bf16[4608,1152]{1,0:T(8,128)(2,1)}, f32[1,3072]{1,0:T(1,128)}, f32[1,3072]{1,0:T(1,128)}) custom-call(s32[1]{0:T(128)} %bitcast.stage_ref, f32[768,1152]{1,0:T(8,128)} %collective-permute-done.5.refs_0_, f32[1536,1152]{1,0:T(8,128)} %collective-permute-done.11.refs_1_, ...), custom_call_target="tpu_custom_call", output_to_operand_aliasing={{0}: (8, {}), {1}: (9, {})} | custom-call | flops 56623104000 | bytes 172032000 | tf_op jit(solution)/shard_map/logits/pallas_call | solution.py:88
  583.9 3.8 collective-permute-start.24
  588.4 9.0 sort.28
  598.7 9.0 sort.29
  609.2 2.9 copy.21.uk_ref
  616.1 37.0 %distinct_sums.1.srt_ref = bf16[3,8192,1152]{2,1,0:T(8,128)(2,1)} custom-call(s32[2]{0:T(128)} %pad_add_fusion.1.info_ref, s32[8192,1]{1,0:T(8,128)} %copy.21.uk_ref, s32[1,9216]{1,0:T(1,128)} %get-tuple-element.140.key_ref, f32[768,1152]{1,0:T(8,128)} %copy-done, f32[3840,1152]{1,0:T(8,128)} %dynamic-slice_convert_fusion.1.refs_1_, ...), custom_call_target="tpu_custom_call" | custom-call | flops 40000000000 | bytes 42467328 | tf_op jit(solution)/shard_map/distinct_sums/pallas_call | solution.py:275
  653.9 145.2 %grad_remote.1 = (f32[8000,1152]{1,0:T(8,128)}, f32[1,1152]{1,0:T(1,128)}) custom-call(s32[11]{0:T(128)} %copy-done.10, f32[8000,4608]{1,0:T(8,128)} %get-tuple-element.110.lg_ref, bf16[4608,1152]{1,0:T(8,128)(2,1)} %get-tuple-element.111.f_ref, f32[1,4608]{1,0:T(1,128)} %get-tuple-element.133.m_ref, ...), custom_call_target="tpu_custom_call", output_to_operand_aliasing={{0}: (6, {})} | custom-call | flops 84934656000 | bytes 221184000 | tf_op jit(solution)/shard_map/grad_remote/pallas_call | solution.py:203
  800.4 55.0 %psum.7 = f32[]{:T(128)} all-reduce(f32[]{:T(128)} %reduce_sum.19), channel_id=1, replica_groups=mesh['tp'=2,'dp'=2,'pp'=2] {'tp','pp'}, use_global_device_ids=true, to_apply=%region_4.5 | all-reduce | flops 1 | bytes 8 | tf_op jit(solution)/shard_map/psum | solution.py:445
  856.2 94.3 %adamw.2 = (f32[16000,1152]{1,0:T(8,128)}, f32[16000,1152]{1,0:T(8,128)}, f32[16000,1152]{1,0:T(8,128)}, bf16[16000,1152]{1,0:T(8,128)(2,1)}) custom-call(s32[1]{0:T(128)S(6)} %mul.66.off_ref, f32[1]{0:T(128)} %bitcast.8.scale_ref, f32[16000,1152]{1,0:T(8,128)} %e_ref.3, f32[16000,1152]{1,0:T(8,128)} %m_ref.3, f32[16000,1152]{1,0:T(8,128)} %v_ref.3, ...), custom_call_target="tpu_custom_call" | custom-call | flops 80000000000 | bytes 276480000 | tf_op jit(solution)/shard_map/adamw/pallas_call | solution.py:311
  950.5 94.3 %adamw.3 = (f32[16000,1152]{1,0:T(8,128)}, f32[16000,1152]{1,0:T(8,128)}, f32[16000,1152]{1,0:T(8,128)}, bf16[16000,1152]{1,0:T(8,128)(2,1)}) custom-call(s32[1]{0:T(128)S(6)} %mul.52.off_ref, f32[1]{0:T(128)} %bitcast.8.scale_ref, f32[16000,1152]{1,0:T(8,128)} %e_ref.3, ...), custom_call_target="tpu_custom_call", output_to_operand_aliasing={{0}: (6, {}), {1}: (7, {}), {2}: (8, {}), {3}: (9, {})} | custom-call | flops 80000000000 | bytes 276480000 | tf_op jit(solution)/shard_map/adamw/pallas_call | solution.py:311
  (101 shorter events, 30.9 us)
Async XLA Ops:
  23.7 59.9 %collective-permute-start.1 = (f32[3840,1152]{1,0:T(8,128)}, f32[3840,1152]{1,0:T(8,128)}, u32[]{:S(2)}, u32[]{:S(2)}) collective-permute-start(f32[3840,1152]{1,0:T(8,128)} %dynamic-slice_convert_fusion.1.refs_1_), channel_id=1, source_target_pairs={{0,1},{1,0},{2,3},{3,2},{4,5},{5,4},{6,7},{7,6}} | collective-permute-start | bytes 53084168 | tf_op jit(solution)/shard_map/ppermute | solution.py:337
  24.5 31.5 %collective-permute-start.2 = (f32[768,1152]{1,0:T(8,128)S(1)}, f32[768,1152]{1,0:T(8,128)}, u32[]{:S(2)}, u32[]{:S(2)}) collective-permute-start(f32[768,1152]{1,0:T(8,128)S(1)} %dynamic-slice_convert_fusion.5.refs_0_), channel_id=1, source_target_pairs={{0,1},{1,0},{2,3},{3,2},{4,5},{5,4},{6,7},{7,6}} | collective-permute-start | bytes 10616840 | tf_op jit(solution)/shard_map/ppermute | solution.py:337
  24.5 110.3 %collective-permute-start.6 = (f32[1536,1152]{1,0:T(8,128)}, f32[1536,1152]{1,0:T(8,128)}, u32[]{:S(2)}, u32[]{:S(2)}) collective-permute-start(f32[1536,1152]{1,0:T(8,128)} %dynamic-slice_convert_fusion.2), channel_id=1, source_target_pairs={{1,3},{3,1},{5,7},{7,5}} | collective-permute-start | bytes 21233672 | tf_op jit(solution)/shard_map/ppermute | solution.py:337
  28.0 188.7 %collective-permute-start.3 = (s32[1,4608]{1,0:T(1,128)}, s32[1,4608]{1,0:T(1,128)}, u32[]{:S(2)}, u32[]{:S(2)}) collective-permute-start(s32[1,4608]{1,0:T(1,128)} %bitcast.1), channel_id=1, source_target_pairs={{0,2},{1,3},{2,0},{3,1},{4,6},{5,7},{6,4},{7,5}} | collective-permute-start | bytes 55304 | tf_op jit(solution)/shard_map/ppermute | solution.py:337
  31.0 182.2 %collective-permute-start.4 = (s32[1,4608]{1,0:T(1,128)}, s32[1,4608]{1,0:T(1,128)}, u32[]{:S(2)}, u32[]{:S(2)}) collective-permute-start(s32[1,4608]{1,0:T(1,128)} %bitcast.1), channel_id=1, source_target_pairs={{0,3},{1,2},{2,1},{3,0},{4,7},{5,6},{6,5},{7,4}} | collective-permute-start | bytes 55304 | tf_op jit(solution)/shard_map/ppermute | solution.py:337
  56.0 166.1 %collective-permute-start = (s32[1,4608]{1,0:T(1,128)}, s32[1,4608]{1,0:T(1,128)S(1)}, u32[]{:S(2)}, u32[]{:S(2)}) collective-permute-start(s32[1,4608]{1,0:T(1,128)} %bitcast.1), channel_id=1, source_target_pairs={{0,1},{1,0},{2,3},{3,2},{4,5},{5,4},{6,7},{7,6}} | collective-permute-start | bytes 55304 | tf_op jit(solution)/shard_map/ppermute | solution.py:337
  83.6 138.6 %collective-permute-start.5 = (f32[768,1152]{1,0:T(8,128)}, f32[768,1152]{1,0:T(8,128)}, u32[]{:S(2)}, u32[]{:S(2)}) collective-permute-start(f32[768,1152]{1,0:T(8,128)} %dynamic-slice_convert_fusion.6), channel_id=1, source_target_pairs={{1,3},{3,1},{5,7},{7,5}} | collective-permute-start | bytes 10616840 | tf_op jit(solution)/shard_map/ppermute | solution.py:337
  134.8 92.3 %collective-permute-start.7 = (f32[1536,1152]{1,0:T(8,128)}, f32[1536,1152]{1,0:T(8,128)}, u32[]{:S(2)}, u32[]{:S(2)}) collective-permute-start(f32[1536,1152]{1,0:T(8,128)} %collective-permute-done.6.refs_0_), channel_id=1, source_target_pairs={{1,0},{3,2},{5,4},{7,6}} | collective-permute-start | bytes 21233672 | tf_op jit(solution)/shard_map/ppermute | solution.py:337
  213.2 121.0 %collective-permute-start.11 = (f32[1536,1152]{1,0:T(8,128)}, f32[1536,1152]{1,0:T(8,128)}, u32[]{:S(2)}, u32[]{:S(2)}) collective-permute-start(f32[1536,1152]{1,0:T(8,128)} %collective-permute-done.6.refs_0_), channel_id=1, source_target_pairs={{1,5},{3,7},{5,1},{7,3}} | collective-permute-start | bytes 21233672 | tf_op jit(solution)/shard_map/ppermute | solution.py:337
  216.7 62.9 %collective-permute-start.17 = (f32[1152,1152]{1,0:T(8,128)S(1)}, f32[1152,1152]{1,0:T(8,128)S(1)}, u32[]{:S(2)}, u32[]{:S(2)}) collective-permute-start(f32[1152,1152]{1,0:T(8,128)S(1)} %get-tuple-element.137), channel_id=1, source_target_pairs={{0,2},{2,0},{4,6},{6,4}} | collective-permute-start | bytes 15925256 | tf_op jit(solution)/shard_map/ppermute | solution.py:337
  222.2 115.9 %collective-permute-start.10 = (f32[2,4608]{1,0:T(2,128)S(1)}, f32[2,4608]{1,0:T(2,128)S(1)}, u32[]{:S(2)}, u32[]{:S(2)}) collective-permute-start(f32[2,4608]{1,0:T(2,128)S(1)} %pad_maximum_fusion), channel_id=1, source_target_pairs={{0,5},{1,4},{2,7},{3,6},{4,1},{5,0},{6,3},{7,2}} | collective-permute-start | bytes 110600 | tf_op jit(solution)/shard_map/ppermute | solution.py:337
  223.1 109.7 %collective-permute-start.12 = (f32[768,1152]{1,0:T(8,128)}, f32[768,1152]{1,0:T(8,128)}, u32[]{:S(2)}, u32[]{:S(2)}) collective-permute-start(f32[768,1152]{1,0:T(8,128)} %collective-permute-done.5.refs_0_), channel_id=1, source_target_pairs={{1,5},{3,7},{5,1},{7,3}} | collective-permute-start | bytes 10616840 | tf_op jit(solution)/shard_map/ppermute | solution.py:337
  226.5 53.2 %copy-start.2 = (s32[2,9216]{1,0:T(2,128)}, s32[2,9216]{1,0:T(2,128)S(1)}, u32[]{:S(2)}) copy-start(s32[2,9216]{1,0:T(2,128)S(1)} %add_subtract_fusion) | copy-start | bytes 221188
  227.1 111.0 %collective-permute-start.9 = (f32[2,4608]{1,0:T(2,128)S(1)}, f32[2,4608]{1,0:T(2,128)S(1)}, u32[]{:S(2)}, u32[]{:S(2)}) collective-permute-start(f32[2,4608]{1,0:T(2,128)S(1)} %pad_maximum_fusion), channel_id=1, source_target_pairs={{0,4},{1,5},{2,6},{3,7},{4,0},{5,1},{6,2},{7,3}} | collective-permute-start | bytes 110600 | tf_op jit(solution)/shard_map/ppermute | solution.py:337
  282.0 56.1 %collective-permute-start.8 = (f32[2,4608]{1,0:T(2,128)S(1)}, f32[2,4608]{1,0:T(2,128)S(1)}, u32[]{:S(2)}, u32[]{:S(2)}) collective-permute-start(f32[2,4608]{1,0:T(2,128)S(1)} %pad_maximum_fusion), channel_id=1, source_target_pairs={{0,1},{1,0},{2,3},{3,2},{4,5},{5,4},{6,7},{7,6}} | collective-permute-start | bytes 110600 | tf_op jit(solution)/shard_map/ppermute | solution.py:337
  332.8 143.8 %collective-permute-start.13 = (f32[768,1152]{1,0:T(8,128)}, f32[768,1152]{1,0:T(8,128)}, u32[]{:S(2)}, u32[]{:S(2)}) collective-permute-start(f32[768,1152]{1,0:T(8,128)} %collective-permute-done.5.refs_0_), channel_id=1, source_target_pairs={{1,0},{3,2},{5,4},{7,6}} | collective-permute-start | bytes 10616840 | tf_op jit(solution)/shard_map/ppermute | solution.py:337
  334.2 128.9 %collective-permute-start.18 = (f32[1152,1152]{1,0:T(8,128)}, f32[1152,1152]{1,0:T(8,128)}, u32[]{:S(2)}, u32[]{:S(2)}) collective-permute-start(f32[1152,1152]{1,0:T(8,128)} %get-tuple-element.136), channel_id=1, source_target_pairs={{0,2},{2,0},{4,6},{6,4}} | collective-permute-start | bytes 15925256 | tf_op jit(solution)/shard_map/ppermute | solution.py:337
  338.1 142.1 %collective-permute-start.15 = (f32[768,1152]{1,0:T(8,128)}, f32[768,1152]{1,0:T(8,128)}, u32[]{:S(2)}, u32[]{:S(2)}) collective-permute-start(f32[768,1152]{1,0:T(8,128)} %collective-permute-done.12.refs_2_), channel_id=1, source_target_pairs={{1,0},{3,2},{5,4},{7,6}} | collective-permute-start | bytes 10616840 | tf_op jit(solution)/shard_map/ppermute | solution.py:337
  339.4 144.5 %collective-permute-start.19 = (f32[1152,1152]{1,0:T(8,128)}, f32[1152,1152]{1,0:T(8,128)}, u32[]{:S(2)}, u32[]{:S(2)}) collective-permute-start(f32[1152,1152]{1,0:T(8,128)} %copy-done.11), channel_id=1, source_target_pairs={{0,4},{2,6},{4,0},{6,2}} | collective-permute-start | bytes 15925256 | tf_op jit(solution)/shard_map/ppermute | solution.py:337
  342.8 144.7 %collective-permute-start.14 = (f32[1536,1152]{1,0:T(8,128)}, f32[1536,1152]{1,0:T(8,128)}, u32[]{:S(2)}, u32[]{:S(2)}) collective-permute-start(f32[1536,1152]{1,0:T(8,128)} %collective-permute-done.11.refs_1_), channel_id=1, source_target_pairs={{1,0},{3,2},{5,4},{7,6}} | collective-permute-start | bytes 21233672 | tf_op jit(solution)/shard_map/ppermute | solution.py:337
  463.0 151.2 %collective-permute-start.22 = (f32[1152,1152]{1,0:T(8,128)}, f32[1152,1152]{1,0:T(8,128)}, u32[]{:S(2)}, u32[]{:S(2)}) collective-permute-start(f32[1152,1152]{1,0:T(8,128)} %collective-permute-done.18.refs_3_), channel_id=1, source_target_pairs={{0,1},{2,3},{4,5},{6,7}} | collective-permute-start | bytes 15925256 | tf_op jit(solution)/shard_map/ppermute | solution.py:337
  476.6 107.2 %collective-permute-start.20 = (f32[1152,1152]{1,0:T(8,128)}, f32[1152,1152]{1,0:T(8,128)}, u32[]{:S(2)}, u32[]{:S(2)}) collective-permute-start(f32[1152,1152]{1,0:T(8,128)} %collective-permute-done.18.refs_3_), channel_id=1, source_target_pairs={{0,4},{2,6},{4,0},{6,2}} | collective-permute-start | bytes 15925256 | tf_op jit(solution)/shard_map/ppermute | solution.py:337
  480.3 134.3 %collective-permute-start.21 = (f32[1152,1152]{1,0:T(8,128)}, f32[1152,1152]{1,0:T(8,128)}, u32[]{:S(2)}, u32[]{:S(2)}) collective-permute-start(f32[1152,1152]{1,0:T(8,128)} %copy-done.11), channel_id=1, source_target_pairs={{0,1},{2,3},{4,5},{6,7}} | collective-permute-start | bytes 15925256 | tf_op jit(solution)/shard_map/ppermute | solution.py:337
  483.9 132.2 %collective-permute-start.23 = (f32[1152,1152]{1,0:T(8,128)}, f32[1152,1152]{1,0:T(8,128)}, u32[]{:S(2)}, u32[]{:S(2)}) collective-permute-start(f32[1152,1152]{1,0:T(8,128)} %collective-permute-done.19.refs_4_), channel_id=1, source_target_pairs={{0,1},{2,3},{4,5},{6,7}} | collective-permute-start | bytes 15925256 | tf_op jit(solution)/shard_map/ppermute | solution.py:337
  487.6 100.1 %copy-start.3 = (s32[2,9216]{1,0:T(2,128)S(1)}, s32[2,9216]{1,0:T(2,128)}, u32[]{:S(2)}) copy-start(s32[2,9216]{1,0:T(2,128)} %copy-done.2) | copy-start | bytes 221188
  487.6 125.1 %copy-start.8 = (f32[1,1536]{1,0:T(1,128)S(1)}, f32[1,1536]{1,0:T(1,128)}, u32[]{:S(2)}) copy-start(f32[1,1536]{1,0:T(1,128)} %get-tuple-element.89) | copy-start | bytes 18436
  487.6 125.1 %copy-start.9 = (f32[1,1536]{1,0:T(1,128)S(1)}, f32[1,1536]{1,0:T(1,128)}, u32[]{:S(2)}) copy-start(f32[1,1536]{1,0:T(1,128)} %get-tuple-element.113) | copy-start | bytes 18436
  583.9 32.2 %collective-permute-start.24 = (f32[1152,1152]{1,0:T(8,128)}, f32[1152,1152]{1,0:T(8,128)}, u32[]{:S(2)}, u32[]{:S(2)}) collective-permute-start(f32[1152,1152]{1,0:T(8,128)} %collective-permute-done.20.refs_5_), channel_id=1, source_target_pairs={{0,1},{2,3},{4,5},{6,7}} | collective-permute-start | bytes 15925256 | tf_op jit(solution)/shard_map/ppermute | solution.py:337
  614.2 38.9 %collective-permute-start.26 = (f32[2,4608]{1,0:T(2,128)S(1)}, f32[2,4608]{1,0:T(2,128)S(1)}, u32[]{:S(2)}, u32[]{:S(2)}) collective-permute-start(f32[2,4608]{1,0:T(2,128)S(1)} %pad_maximum_fusion.1), channel_id=1, source_target_pairs={{0,5},{1,4},{2,7},{3,6},{4,1},{5,0},{6,3},{7,2}} | collective-permute-start | bytes 110600 | tf_op jit(solution)/shard_map/ppermute | solution.py:337
  614.2 38.9 %collective-permute-start.25 = (f32[2,4608]{1,0:T(2,128)S(1)}, f32[2,4608]{1,0:T(2,128)S(1)}, u32[]{:S(2)}, u32[]{:S(2)}) collective-permute-start(f32[2,4608]{1,0:T(2,128)S(1)} %pad_maximum_fusion.1), channel_id=1, source_target_pairs={{0,4},{1,5},{2,6},{3,7},{4,0},{5,1},{6,2},{7,3}} | collective-permute-start | bytes 110600 | tf_op jit(solution)/shard_map/ppermute | solution.py:337
  614.6 38.6 %collective-permute-start.16 = (f32[2,4608]{1,0:T(2,128)S(1)}, f32[2,4608]{1,0:T(2,128)S(1)}, u32[]{:S(2)}, u32[]{:S(2)}) collective-permute-start(f32[2,4608]{1,0:T(2,128)S(1)} %pad_maximum_fusion.1), channel_id=1, source_target_pairs={{0,1},{1,0},{2,3},{3,2},{4,5},{5,4},{6,7},{7,6}} | collective-permute-start | bytes 110600 | tf_op jit(solution)/shard_map/ppermute | solution.py:337
  799.1 151.4 %collective-permute-start.27 = (f32[8000,1152]{1,0:T(8,128)}, f32[8000,1152]{1,0:T(8,128)}, u32[]{:S(2)}, u32[]{:S(2)}) collective-permute-start(f32[8000,1152]{1,0:T(8,128)} %get-tuple-element.127.g_ref), channel_id=1, source_target_pairs={{0,1},{1,0},{2,3},{3,2},{4,5},{5,4},{6,7},{7,6}} | collective-permute-start | bytes 110592008 | tf_op jit(solution)/shard_map/ppermute | solution.py:337
  (8 other events, 163.2 us)
where the time goes:
time: 1050 us
  Pallas kernels  782 us (74%)
  starting transfers between devices  66.7 us (6%)
  waiting for transfers between devices  56 us (5%)
  blocking collectives  55 us (5%)
  other arithmetic  52.8 us (5%)
  local copies, waits for them, and re-layouts  29.2 us (3%)
    pallas_call x5, Pallas kernels, logits_call(): pl.pallas_call(functools.partial(logits_kernel, n_sub, starts), grid_spec...  294 us
    pallas_call x2, Pallas kernels, adamw_call(): pl.pallas_call(adamw_kernel, grid_spec=pltpu.PrefetchScalarGridSpec(num_s...  189 us
    pallas_call x1, Pallas kernels, grad_call(): pl.pallas_call(functools.partial(grad_remote_kernel, unit, k_width, n_pre...  145 us
    pallas_call x1, Pallas kernels, grad_call(): pl.pallas_call(functools.partial(grad_local_kernel, unit, k_width), grid=...  118 us
    ppermute x28, starting transfers between devices, permute(): return lax.ppermute(x, AXES, pairs)  66.7 us
    ppermute x28, waiting for transfers between devices, permute(): return lax.ppermute(x, AXES, pairs)  56 us
    psum x1, blocking collectives, stage_step(): sq_total = lax.psum(jnp.sum(sq), ('tp', 'pp')) * 0.25  55 us
    pallas_call x1, Pallas kernels, distinct_call(): pl.pallas_call(functools.partial(distinct_kernel, n_stage_rows, blocks),...  37 us
  transfers between devices with their start and end apart: 28, of which 2 were waited for; matrix products, arithmetic and copies ran while one was open for 5% of the time, Pallas kernels for 52%

commit v1 on v0

--- a/solution.py
+++ b/solution.py
@@ -15,7 +15,7 @@
 WEIGHT_DECAY = 0.1
 CLIP_NORM = 1.0
 OPT_STEP = 10
-VMEM_CAP = 63 * 1024 * 1024
+VMEM_CAP = 67043328
 F32 = jnp.float32
 BF16 = jnp.bfloat16
 AXES = ("tp", "dp", "pp")
@@ -199,7 +199,7 @@
             name="grad_local",
         )(lg, f_bf, peak, weight, lab)
     offs, g_in, keys, srt, chunk = extra
-    n_pre = 3
+    n_pre = 2
     return pl.pallas_call(
         functools.partial(grad_remote_kernel, unit, k_width, n_pre),
         grid_spec=pltpu.PrefetchScalarGridSpec(
@@ -373,7 +373,7 @@
         half = tok // 2
         tb = tok // 6
         dxb = half // 2
-        vb1, vb2, vb3 = vq // 5, vq // 10, vq // 20
+        vb1, vb2, vb3 = vq // 4, vq // 10, vq // 20
         chunk = 256
         stage = pp.astype(jnp.int32).reshape(1)
         act = stage_acts.reshape(tok, d)
@@ -426,7 +426,7 @@
         dy0, dxs0 = permute(dx0, "tp", 0), permute(dx0, "pp", 0)
         unit = 1.0 / tok
         lg_loc = after(lg_c[0], fr_a[2])
-        g_loc = grad_call(lg_loc, lg_c[1], m_loc, unit / z_loc, all_ids[1:2, :tok], unit, vb2, tok // 2, tb)
+        g_loc = grad_call(lg_loc, lg_c[1], m_loc, unit / z_loc, all_ids[1:2, :tok], unit, vb2, tok, tb)
         dx1 = after(dx[1], g_loc)
         dy1, dxs1 = permute(dx1, "tp", 0), permute(dx1, "pp", 0)
         dys0 = permute(after(dy0, g_loc), "pp", 0)
@@ -439,11 +439,11 @@
         sums = distinct_call(info, uk.reshape(-1, 1), key.reshape(1, -1), *srcs, chunk, tb // 2)
         m_far, z_far = reduce_stats(*(jnp.concatenate([fr_a[i], fr_b[i]], axis=1) for i in (2, 3)), True, sums)
         extra = (offs, g_loc, uk.reshape(-1, 1, chunk), sums, chunk)
-        grad, sq = grad_call(fr_b[0], fr_b[1], m_far, unit / z_far, all_ids[1:2, tok:], unit, vb2, tok // 2, tb, extra)
-
-        other = permute(grad, "pp")
+        grad, sq = grad_call(fr_b[0], fr_b[1], m_far, unit / z_far, all_ids[1:2, tok:], unit, vb2, tok, tb, extra)
+
         sq_total = lax.psum(jnp.sum(sq), ("tp", "pp")) * 0.25
         scale = (0.5 * (CLIP_NORM / jnp.maximum(jnp.sqrt(sq_total), CLIP_NORM))).reshape(1)
+        other = permute(after(grad, scale), "pp")
         n_blk = vq // vb3
         outs = adamw_call(stage * n_blk, scale, master, exp_avg, exp_avg_sq, grad, vb3, None)
         return tuple(adamw_call((1 - stage) * n_blk, scale, master, exp_avg, exp_avg_sq, other, vb3, outs))

time: 1050 us -> 1000 us (0.952)
  blocking collectives: 55 us -> 6.56 us
    psum x1, blocking collectives: 55 us -> 6.56 us  [stage_step(): sq_total = lax.psum(jnp.sum(sq), ('tp', 'pp')) * 0.25]
  transfers between devices with their start and end apart: 28 -> 28, of which waited for: 2 -> 2; matrix products, arithmetic and copies ran while one was open for 5% -> 6% of each run, Pallas kernels for 52% -> 54%
where the time goes in v1:
time: 1000 us; the launch traced here: 997 us
  Pallas kernels  775 us (78%)
  starting transfers between devices  67.7 us (7%)
  other arithmetic  56.7 us (6%)
  waiting for transfers between devices  55.1 us (6%)
  local copies, waits for them, and re-layouts  33 us (3%)
    pallas_call x5, Pallas kernels, logits_call(): pl.pallas_call(functools.partial(logits_kernel, n_sub, starts), grid_spec...  288 us
    pallas_call x2, Pallas kernels, adamw_call(): pl.pallas_call(adamw_kernel, grid_spec=pltpu.PrefetchScalarGridSpec(num_s...  189 us
    pallas_call x1, Pallas kernels, grad_call(): pl.pallas_call(functools.partial(grad_remote_kernel, unit, k_width, n_pre...  145 us
    pallas_call x1, Pallas kernels, grad_call(): pl.pallas_call(functools.partial(grad_local_kernel, unit, k_width), grid=...  116 us
    ppermute x28, starting transfers between devices, permute(): return lax.ppermute(x, AXES, pairs)  67.7 us
    ppermute x28, waiting for transfers between devices, permute(): return lax.ppermute(x, AXES, pairs)  55.1 us
    pallas_call x1, Pallas kernels, distinct_call(): pl.pallas_call(functools.partial(distinct_kernel, n_stage_rows, blocks),...  37 us
    convert_element_type x5, other arithmetic, part(): return lax.dynamic_slice(source, (start, 0), (size, d)).astype(F32)  28.6 us
  transfers between devices with their start and end apart: 28, of which 2 were waited for; matrix products, arithmetic and copies ran while one was open for 6% of the time, Pallas kernels for 54%

profile of v1, /device:TPU:0, one launch (start us, length us, event | category | flops | bytes accessed | tf_op | source)
XLA Modules:
  0.0 997.1 jit_solution(180089039687775659)
XLA Ops:
  0.6 5.4 dynamic-slice_convert_fusion.2
  6.1 3.5 dynamic-slice_convert_fusion.6
  11.3 12.4 %dynamic-slice_convert_fusion.1.refs_1_ = f32[3840,1152]{1,0:T(8,128)} fusion(bf16[4608,1152]{1,0:T(8,128)(2,1)} %bitcast.12, s32[]{:T(128)S(6)} %select_n.66), kind=kLoop, calls=%fused_computation.1 | loop fusion | flops 4423680 | bytes 26542084 | tf_op jit(solution)/shard_map/convert_element_type | solution.py:383
  24.5 3.5 collective-permute-start.6
  28.0 3.0 collective-permute-start.3
  31.0 19.9 %dynamic-slice_convert_fusion.refs_2_.refs_6_ = bf16[8000,1152]{1,0:T(8,128)(2,1)} fusion(f32[16000,1152]{1,0:T(8,128)} %e_ref.3, s32[]{:T(128)S(6)} %select_n.67), kind=kLoop, calls=%fused_computation | loop fusion | bytes 36864004 | tf_op jit(solution)/shard_map/convert_element_type | solution.py:390
  50.9 5.1 collective-permute-done.2.refs_1_.refs_6_
  56.4 26.9 %logits.5 = (f32[8000,4608]{1,0:T(8,128)}, bf16[4608,1152]{1,0:T(8,128)(2,1)}, f32[1,768]{1,0:T(1,128)}, f32[1,768]{1,0:T(1,128)}) custom-call(s32[1]{0:T(128)} %bitcast.stage_ref, bf16[4608,1152]{1,0:T(8,128)(2,1)} %bitcast.13, f32[768,1152]{1,0:T(8,128)} %collective-permute-done.2.refs_1_.refs_6_, bf16[8000,1152]{1,0:T(8,128)(2,1)} %dynamic-slice_convert_fusion.refs_2_.refs_6_), custom_call_target="tpu_custom_call" | custom-call | flops 14155776000 | bytes 43008000 | tf_op jit(solution)/shard_map/logits/pallas_call | solution.py:88
  87.2 47.8 %logits.6 = (f32[8000,4608]{1,0:T(8,128)}, bf16[4608,1152]{1,0:T(8,128)(2,1)}, f32[1,1536]{1,0:T(1,128)}, f32[1,1536]{1,0:T(1,128)}) custom-call(s32[1]{0:T(128)} %bitcast.stage_ref, bf16[4608,1152]{1,0:T(8,128)(2,1)} %bitcast.14, f32[3840,1152]{1,0:T(8,128)} %collective-permute-done.1.refs_1_.refs_7_, ...), custom_call_target="tpu_custom_call", output_to_operand_aliasing={{0}: (4, {}), {1}: (5, {})} | custom-call | flops 28311552000 | bytes 86016000 | tf_op jit(solution)/shard_map/logits/pallas_call | solution.py:88
  136.2 69.0 %logits.7 = (f32[8000,4608]{1,0:T(8,128)}, bf16[4608,1152]{1,0:T(8,128)(2,1)}, f32[1,2304]{1,0:T(1,128)}, f32[1,2304]{1,0:T(1,128)}) custom-call(s32[1]{0:T(128)} %bitcast.stage_ref, bf16[4608,1152]{1,0:T(8,128)(2,1)} %bitcast.15, f32[3840,1152]{1,0:T(8,128)} %collective-permute-done.1.refs_1_.refs_7_, ...), custom_call_target="tpu_custom_call", output_to_operand_aliasing={{0}: (4, {}), {1}: (5, {})} | custom-call | flops 42467328000 | bytes 129024000 | tf_op jit(solution)/shard_map/logits/pallas_call | solution.py:88
  205.3 5.6 dynamic-slice_convert_fusion.3
  210.9 3.5 collective-permute-start.11
  214.4 4.7 collective-permute-start.17
  227.4 49.9 %collective-permute-done.17.refs_2_ = f32[1152,1152]{1,0:T(8,128)S(1)} collective-permute-done((f32[1152,1152]{1,0:T(8,128)S(1)}, f32[1152,1152]{1,0:T(8,128)S(1)}, u32[]{:S(2)}, u32[]{:S(2)}) %collective-permute-start.17) | collective-permute-done | bytes 5308448 | tf_op jit(solution)/shard_map/ppermute | solution.py:337
  279.7 49.8 %logits.8 = (f32[8000,4608]{1,0:T(8,128)}, bf16[4608,1152]{1,0:T(8,128)(2,1)}, f32[1,1536]{1,0:T(1,128)}, f32[1,1536]{1,0:T(1,128)}) custom-call(s32[1]{0:T(128)} %bitcast.stage_ref, f32[1536,1152]{1,0:T(8,128)} %collective-permute-done.6.refs_0_, f32[1536,1152]{1,0:T(8,128)} %collective-permute-done.7.refs_1_, ...), custom_call_target="tpu_custom_call" | custom-call | flops 28311552000 | bytes 86016000 | tf_op jit(solution)/shard_map/logits/pallas_call | solution.py:88
  330.9 3.9 collective-permute-start.18
  336.2 3.4 collective-permute-start.19
  342.6 116.3 %grad_local.1.gin_ref = f32[8000,1152]{1,0:T(8,128)} custom-call(f32[8000,4608]{1,0:T(8,128)} %get-tuple-element.91.lg_ref, bf16[4608,1152]{1,0:T(8,128)(2,1)} %get-tuple-element.92.f_ref, f32[1,4608]{1,0:T(1,128)} %get-tuple-element.137.m_ref, f32[1,4608]{1,0:T(1,128)} %get-tuple-element.136.w_ref, s32[1,4608]{1,0:T(1,128)} %get-tuple-element.141.lab_ref), custom_call_target="tpu_custom_call" | custom-call | flops 84934656000 | bytes 221184000 | tf_op jit(solution)/shard_map/grad_local/pallas_call | solution.py:191
  458.8 14.6 %collective-permute-start.22 = (f32[1152,1152]{1,0:T(8,128)}, f32[1152,1152]{1,0:T(8,128)}, u32[]{:S(2)}, u32[]{:S(2)}) collective-permute-start(f32[1152,1152]{1,0:T(8,128)} %collective-permute-done.18.refs_3_), channel_id=1, source_target_pairs={{0,1},{2,3},{4,5},{6,7}} | collective-permute-start | bytes 15925256 | tf_op jit(solution)/shard_map/ppermute | solution.py:337
  473.4 3.6 collective-permute-start.20
  477.1 3.6 collective-permute-start.21
  480.7 4.0 collective-permute-start.23
  484.8 94.8 %logits.9 = (f32[8000,4608]{1,0:T(8,128)}, bf16[4608,1152]{1,0:T(8,128)(2,1)}, f32[1,3072]{1,0:T(1,128)}, f32[1,3072]{1,0:T(1,128)}) custom-call(s32[1]{0:T(128)} %bitcast.stage_ref, f32[768,1152]{1,0:T(8,128)} %collective-permute-done.5.refs_0_, f32[1536,1152]{1,0:T(8,128)} %collective-permute-done.11.refs_1_, ...), custom_call_target="tpu_custom_call", output_to_operand_aliasing={{0}: (8, {}), {1}: (9, {})} | custom-call | flops 56623104000 | bytes 172032000 | tf_op jit(solution)/shard_map/logits/pallas_call | solution.py:88
  579.6 3.8 collective-permute-start.24
  584.9 9.0 sort.28
  595.2 9.0 sort.29
  606.2 2.9 copy.21.uk_ref
  615.0 37.0 %distinct_sums.1.srt_ref = bf16[3,8192,1152]{2,1,0:T(8,128)(2,1)} custom-call(s32[2]{0:T(128)} %pad_add_fusion.1.info_ref, s32[8192,1]{1,0:T(8,128)} %copy.21.uk_ref, s32[1,9216]{1,0:T(1,128)} %get-tuple-element.142.key_ref, f32[768,1152]{1,0:T(8,128)} %copy-done, f32[3840,1152]{1,0:T(8,128)} %dynamic-slice_convert_fusion.1.refs_1_, ...), custom_call_target="tpu_custom_call" | custom-call | flops 40000000000 | bytes 42467328 | tf_op jit(solution)/shard_map/distinct_sums/pallas_call | solution.py:275
  655.1 144.5 %grad_remote.1 = (f32[8000,1152]{1,0:T(8,128)}, f32[1,1152]{1,0:T(1,128)}) custom-call(s32[11]{0:T(128)} %copy-done.13, f32[8000,4608]{1,0:T(8,128)} %get-tuple-element.111.lg_ref, bf16[4608,1152]{1,0:T(8,128)(2,1)} %get-tuple-element.112.f_ref, f32[1,4608]{1,0:T(1,128)} %get-tuple-element.135.m_ref, ...), custom_call_target="tpu_custom_call", output_to_operand_aliasing={{0}: (6, {})} | custom-call | flops 84934656000 | bytes 221184000 | tf_op jit(solution)/shard_map/grad_remote/pallas_call | solution.py:203
  801.0 6.6 psum.7
  808.3 94.3 %adamw.2 = (f32[16000,1152]{1,0:T(8,128)}, f32[16000,1152]{1,0:T(8,128)}, f32[16000,1152]{1,0:T(8,128)}, bf16[16000,1152]{1,0:T(8,128)(2,1)}) custom-call(s32[1]{0:T(128)S(6)} %mul.66.off_ref, f32[1]{0:T(128)} %bitcast.8.scale_ref, f32[16000,1152]{1,0:T(8,128)} %e_ref.3, f32[16000,1152]{1,0:T(8,128)} %m_ref.3, f32[16000,1152]{1,0:T(8,128)} %v_ref.3, ...), custom_call_target="tpu_custom_call" | custom-call | flops 80000000000 | bytes 276480000 | tf_op jit(solution)/shard_map/adamw/pallas_call | solution.py:311
  902.6 94.3 %adamw.3 = (f32[16000,1152]{1,0:T(8,128)}, f32[16000,1152]{1,0:T(8,128)}, f32[16000,1152]{1,0:T(8,128)}, bf16[16000,1152]{1,0:T(8,128)(2,1)}) custom-call(s32[1]{0:T(128)S(6)} %mul.52.off_ref, f32[1]{0:T(128)} %bitcast.8.scale_ref, f32[16000,1152]{1,0:T(8,128)} %e_ref.3, ...), custom_call_target="tpu_custom_call", output_to_operand_aliasing={{0}: (6, {}), {1}: (7, {}), {2}: (8, {}), {3}: (9, {})} | custom-call | flops 80000000000 | bytes 276480000 | tf_op jit(solution)/shard_map/adamw/pallas_call | solution.py:311
  (107 shorter events, 38.2 us)
Async XLA Ops:
  23.7 60.9 %collective-permute-start.1 = (f32[3840,1152]{1,0:T(8,128)}, f32[3840,1152]{1,0:T(8,128)}, u32[]{:S(2)}, u32[]{:S(2)}) collective-permute-start(f32[3840,1152]{1,0:T(8,128)} %dynamic-slice_convert_fusion.1.refs_1_), channel_id=1, source_target_pairs={{0,1},{1,0},{2,3},{3,2},{4,5},{5,4},{6,7},{7,6}} | collective-permute-start | bytes 53084168 | tf_op jit(solution)/shard_map/ppermute | solution.py:337
  24.5 31.5 %collective-permute-start.2 = (f32[768,1152]{1,0:T(8,128)S(1)}, f32[768,1152]{1,0:T(8,128)}, u32[]{:S(2)}, u32[]{:S(2)}) collective-permute-start(f32[768,1152]{1,0:T(8,128)S(1)} %dynamic-slice_convert_fusion.5.refs_0_), channel_id=1, source_target_pairs={{0,1},{1,0},{2,3},{3,2},{4,5},{5,4},{6,7},{7,6}} | collective-permute-start | bytes 10616840 | tf_op jit(solution)/shard_map/ppermute | solution.py:337
  24.5 110.4 %collective-permute-start.6 = (f32[1536,1152]{1,0:T(8,128)}, f32[1536,1152]{1,0:T(8,128)}, u32[]{:S(2)}, u32[]{:S(2)}) collective-permute-start(f32[1536,1152]{1,0:T(8,128)} %dynamic-slice_convert_fusion.2), channel_id=1, source_target_pairs={{1,3},{3,1},{5,7},{7,5}} | collective-permute-start | bytes 21233672 | tf_op jit(solution)/shard_map/ppermute | solution.py:337
  28.0 186.4 %collective-permute-start.3 = (s32[1,4608]{1,0:T(1,128)}, s32[1,4608]{1,0:T(1,128)}, u32[]{:S(2)}, u32[]{:S(2)}) collective-permute-start(s32[1,4608]{1,0:T(1,128)} %bitcast.1), channel_id=1, source_target_pairs={{0,2},{1,3},{2,0},{3,1},{4,6},{5,7},{6,4},{7,5}} | collective-permute-start | bytes 55304 | tf_op jit(solution)/shard_map/ppermute | solution.py:337
  31.0 179.9 %collective-permute-start.4 = (s32[1,4608]{1,0:T(1,128)}, s32[1,4608]{1,0:T(1,128)}, u32[]{:S(2)}, u32[]{:S(2)}) collective-permute-start(s32[1,4608]{1,0:T(1,128)} %bitcast.1), channel_id=1, source_target_pairs={{0,3},{1,2},{2,1},{3,0},{4,7},{5,6},{6,5},{7,4}} | collective-permute-start | bytes 55304 | tf_op jit(solution)/shard_map/ppermute | solution.py:337
  56.0 164.7 %collective-permute-start = (s32[1,4608]{1,0:T(1,128)}, s32[1,4608]{1,0:T(1,128)}, u32[]{:S(2)}, u32[]{:S(2)}) collective-permute-start(s32[1,4608]{1,0:T(1,128)} %bitcast.1), channel_id=1, source_target_pairs={{0,1},{1,0},{2,3},{3,2},{4,5},{5,4},{6,7},{7,6}} | collective-permute-start | bytes 55304 | tf_op jit(solution)/shard_map/ppermute | solution.py:337
  84.5 136.2 %collective-permute-start.5 = (f32[768,1152]{1,0:T(8,128)}, f32[768,1152]{1,0:T(8,128)}, u32[]{:S(2)}, u32[]{:S(2)}) collective-permute-start(f32[768,1152]{1,0:T(8,128)} %dynamic-slice_convert_fusion.6), channel_id=1, source_target_pairs={{1,3},{3,1},{5,7},{7,5}} | collective-permute-start | bytes 10616840 | tf_op jit(solution)/shard_map/ppermute | solution.py:337
  134.9 90.8 %collective-permute-start.7 = (f32[1536,1152]{1,0:T(8,128)}, f32[1536,1152]{1,0:T(8,128)}, u32[]{:S(2)}, u32[]{:S(2)}) collective-permute-start(f32[1536,1152]{1,0:T(8,128)} %collective-permute-done.6.refs_0_), channel_id=1, source_target_pairs={{1,0},{3,2},{5,4},{7,6}} | collective-permute-start | bytes 21233672 | tf_op jit(solution)/shard_map/ppermute | solution.py:337
  205.3 14.7 %copy-start.9 = (f32[1,2304]{1,0:T(1,128)S(1)}, f32[1,2304]{1,0:T(1,128)}, u32[]{:S(2)}) copy-start(f32[1,2304]{1,0:T(1,128)} %get-tuple-element.96) | copy-start | bytes 27652
  210.9 120.0 %collective-permute-start.11 = (f32[1536,1152]{1,0:T(8,128)}, f32[1536,1152]{1,0:T(8,128)}, u32[]{:S(2)}, u32[]{:S(2)}) collective-permute-start(f32[1536,1152]{1,0:T(8,128)} %collective-permute-done.6.refs_0_), channel_id=1, source_target_pairs={{1,5},{3,7},{5,1},{7,3}} | collective-permute-start | bytes 21233672 | tf_op jit(solution)/shard_map/ppermute | solution.py:337
  214.4 62.9 %collective-permute-start.17 = (f32[1152,1152]{1,0:T(8,128)S(1)}, f32[1152,1152]{1,0:T(8,128)S(1)}, u32[]{:S(2)}, u32[]{:S(2)}) collective-permute-start(f32[1152,1152]{1,0:T(8,128)S(1)} %get-tuple-element.139), channel_id=1, source_target_pairs={{0,2},{2,0},{4,6},{6,4}} | collective-permute-start | bytes 15925256 | tf_op jit(solution)/shard_map/ppermute | solution.py:337
  220.0 57.4 %copy-start.8 = (f32[1,4608]{1,0:T(1,128)}, f32[1,4608]{1,0:T(1,128)S(1)}, u32[]{:S(2)}) copy-start(f32[1,4608]{1,0:T(1,128)S(1)} %constant_dynamic-update-slice_fusion) | copy-start | bytes 55300
  220.0 57.3 %copy-start.6 = (f32[1,4608]{1,0:T(1,128)}, f32[1,4608]{1,0:T(1,128)S(1)}, u32[]{:S(2)}) copy-start(f32[1,4608]{1,0:T(1,128)S(1)} %constant_dynamic-update-slice_fusion.3) | copy-start | bytes 55300
  220.7 114.1 %collective-permute-start.10 = (f32[2,4608]{1,0:T(2,128)}, f32[2,4608]{1,0:T(2,128)}, u32[]{:S(2)}, u32[]{:S(2)}) collective-permute-start(f32[2,4608]{1,0:T(2,128)} %pad_maximum_fusion), channel_id=1, source_target_pairs={{0,5},{1,4},{2,7},{3,6},{4,1},{5,0},{6,3},{7,2}} | collective-permute-start | bytes 110600 | tf_op jit(solution)/shard_map/ppermute | solution.py:337
  221.6 107.9 %collective-permute-start.12 = (f32[768,1152]{1,0:T(8,128)}, f32[768,1152]{1,0:T(8,128)}, u32[]{:S(2)}, u32[]{:S(2)}) collective-permute-start(f32[768,1152]{1,0:T(8,128)} %collective-permute-done.5.refs_0_), channel_id=1, source_target_pairs={{1,5},{3,7},{5,1},{7,3}} | collective-permute-start | bytes 10616840 | tf_op jit(solution)/shard_map/ppermute | solution.py:337
  225.0 52.4 %copy-start.2 = (s32[2,9216]{1,0:T(2,128)}, s32[2,9216]{1,0:T(2,128)S(1)}, u32[]{:S(2)}) copy-start(s32[2,9216]{1,0:T(2,128)S(1)} %add_subtract_fusion) | copy-start | bytes 221188
  225.7 109.2 %collective-permute-start.9 = (f32[2,4608]{1,0:T(2,128)}, f32[2,4608]{1,0:T(2,128)}, u32[]{:S(2)}, u32[]{:S(2)}) collective-permute-start(f32[2,4608]{1,0:T(2,128)} %pad_maximum_fusion), channel_id=1, source_target_pairs={{0,4},{1,5},{2,6},{3,7},{4,0},{5,1},{6,2},{7,3}} | collective-permute-start | bytes 110600 | tf_op jit(solution)/shard_map/ppermute | solution.py:337
  279.7 55.1 %collective-permute-start.8 = (f32[2,4608]{1,0:T(2,128)}, f32[2,4608]{1,0:T(2,128)}, u32[]{:S(2)}, u32[]{:S(2)}) collective-permute-start(f32[2,4608]{1,0:T(2,128)} %pad_maximum_fusion), channel_id=1, source_target_pairs={{0,1},{1,0},{2,3},{3,2},{4,5},{5,4},{6,7},{7,6}} | collective-permute-start | bytes 110600 | tf_op jit(solution)/shard_map/ppermute | solution.py:337
  329.6 143.9 %collective-permute-start.13 = (f32[768,1152]{1,0:T(8,128)}, f32[768,1152]{1,0:T(8,128)}, u32[]{:S(2)}, u32[]{:S(2)}) collective-permute-start(f32[768,1152]{1,0:T(8,128)} %collective-permute-done.5.refs_0_), channel_id=1, source_target_pairs={{1,0},{3,2},{5,4},{7,6}} | collective-permute-start | bytes 10616840 | tf_op jit(solution)/shard_map/ppermute | solution.py:337
  330.9 127.9 %collective-permute-start.18 = (f32[1152,1152]{1,0:T(8,128)}, f32[1152,1152]{1,0:T(8,128)}, u32[]{:S(2)}, u32[]{:S(2)}) collective-permute-start(f32[1152,1152]{1,0:T(8,128)} %get-tuple-element.138), channel_id=1, source_target_pairs={{0,2},{2,0},{4,6},{6,4}} | collective-permute-start | bytes 15925256 | tf_op jit(solution)/shard_map/ppermute | solution.py:337
  334.9 142.2 %collective-permute-start.15 = (f32[768,1152]{1,0:T(8,128)}, f32[768,1152]{1,0:T(8,128)}, u32[]{:S(2)}, u32[]{:S(2)}) collective-permute-start(f32[768,1152]{1,0:T(8,128)} %collective-permute-done.12.refs_2_), channel_id=1, source_target_pairs={{1,0},{3,2},{5,4},{7,6}} | collective-permute-start | bytes 10616840 | tf_op jit(solution)/shard_map/ppermute | solution.py:337
  336.2 144.6 %collective-permute-start.19 = (f32[1152,1152]{1,0:T(8,128)}, f32[1152,1152]{1,0:T(8,128)}, u32[]{:S(2)}, u32[]{:S(2)}) collective-permute-start(f32[1152,1152]{1,0:T(8,128)} %copy-done.14), channel_id=1, source_target_pairs={{0,4},{2,6},{4,0},{6,2}} | collective-permute-start | bytes 15925256 | tf_op jit(solution)/shard_map/ppermute | solution.py:337
  339.6 145.2 %collective-permute-start.14 = (f32[1536,1152]{1,0:T(8,128)}, f32[1536,1152]{1,0:T(8,128)}, u32[]{:S(2)}, u32[]{:S(2)}) collective-permute-start(f32[1536,1152]{1,0:T(8,128)} %collective-permute-done.11.refs_1_), channel_id=1, source_target_pairs={{1,0},{3,2},{5,4},{7,6}} | collective-permute-start | bytes 21233672 | tf_op jit(solution)/shard_map/ppermute | solution.py:337
  458.8 154.3 %collective-permute-start.22 = (f32[1152,1152]{1,0:T(8,128)}, f32[1152,1152]{1,0:T(8,128)}, u32[]{:S(2)}, u32[]{:S(2)}) collective-permute-start(f32[1152,1152]{1,0:T(8,128)} %collective-permute-done.18.refs_3_), channel_id=1, source_target_pairs={{0,1},{2,3},{4,5},{6,7}} | collective-permute-start | bytes 15925256 | tf_op jit(solution)/shard_map/ppermute | solution.py:337
  473.4 106.1 %collective-permute-start.20 = (f32[1152,1152]{1,0:T(8,128)}, f32[1152,1152]{1,0:T(8,128)}, u32[]{:S(2)}, u32[]{:S(2)}) collective-permute-start(f32[1152,1152]{1,0:T(8,128)} %collective-permute-done.18.refs_3_), channel_id=1, source_target_pairs={{0,4},{2,6},{4,0},{6,2}} | collective-permute-start | bytes 15925256 | tf_op jit(solution)/shard_map/ppermute | solution.py:337
  477.1 136.4 %collective-permute-start.21 = (f32[1152,1152]{1,0:T(8,128)}, f32[1152,1152]{1,0:T(8,128)}, u32[]{:S(2)}, u32[]{:S(2)}) collective-permute-start(f32[1152,1152]{1,0:T(8,128)} %copy-done.14), channel_id=1, source_target_pairs={{0,1},{2,3},{4,5},{6,7}} | collective-permute-start | bytes 15925256 | tf_op jit(solution)/shard_map/ppermute | solution.py:337
  480.7 134.3 %collective-permute-start.23 = (f32[1152,1152]{1,0:T(8,128)}, f32[1152,1152]{1,0:T(8,128)}, u32[]{:S(2)}, u32[]{:S(2)}) collective-permute-start(f32[1152,1152]{1,0:T(8,128)} %collective-permute-done.19.refs_4_), channel_id=1, source_target_pairs={{0,1},{2,3},{4,5},{6,7}} | collective-permute-start | bytes 15925256 | tf_op jit(solution)/shard_map/ppermute | solution.py:337
  579.6 35.5 %collective-permute-start.24 = (f32[1152,1152]{1,0:T(8,128)}, f32[1152,1152]{1,0:T(8,128)}, u32[]{:S(2)}, u32[]{:S(2)}) collective-permute-start(f32[1152,1152]{1,0:T(8,128)} %collective-permute-done.20.refs_5_), channel_id=1, source_target_pairs={{0,1},{2,3},{4,5},{6,7}} | collective-permute-start | bytes 15925256 | tf_op jit(solution)/shard_map/ppermute | solution.py:337
  613.2 38.9 %collective-permute-start.26 = (f32[2,4608]{1,0:T(2,128)}, f32[2,4608]{1,0:T(2,128)}, u32[]{:S(2)}, u32[]{:S(2)}) collective-permute-start(f32[2,4608]{1,0:T(2,128)} %pad_maximum_fusion.1), channel_id=1, source_target_pairs={{0,5},{1,4},{2,7},{3,6},{4,1},{5,0},{6,3},{7,2}} | collective-permute-start | bytes 110600 | tf_op jit(solution)/shard_map/ppermute | solution.py:337
  613.2 39.6 %collective-permute-start.25 = (f32[2,4608]{1,0:T(2,128)}, f32[2,4608]{1,0:T(2,128)}, u32[]{:S(2)}, u32[]{:S(2)}) collective-permute-start(f32[2,4608]{1,0:T(2,128)} %pad_maximum_fusion.1), channel_id=1, source_target_pairs={{0,4},{1,5},{2,6},{3,7},{4,0},{5,1},{6,2},{7,3}} | collective-permute-start | bytes 110600 | tf_op jit(solution)/shard_map/ppermute | solution.py:337
  613.5 40.0 %collective-permute-start.16 = (f32[2,4608]{1,0:T(2,128)}, f32[2,4608]{1,0:T(2,128)}, u32[]{:S(2)}, u32[]{:S(2)}) collective-permute-start(f32[2,4608]{1,0:T(2,128)} %pad_maximum_fusion.1), channel_id=1, source_target_pairs={{0,1},{1,0},{2,3},{3,2},{4,5},{5,4},{6,7},{7,6}} | collective-permute-start | bytes 110600 | tf_op jit(solution)/shard_map/ppermute | solution.py:337
  808.3 94.3 %collective-permute-start.27 = (f32[8000,1152]{1,0:T(8,128)}, f32[8000,1152]{1,0:T(8,128)}, u32[]{:S(2)}, u32[]{:S(2)}) collective-permute-start(f32[8000,1152]{1,0:T(8,128)} %get-tuple-element.129.g_ref), channel_id=1, source_target_pairs={{0,1},{1,0},{2,3},{3,2},{4,5},{5,4},{6,7},{7,6}} | collective-permute-start | bytes 110592008 | tf_op jit(solution)/shard_map/ppermute | solution.py:337
  (11 other events, 92.7 us)
